TPU v7x, 32 devices: a whole 2x2x4 slice. The times are simulated.
32 devices in a mesh: centre: 4 (over y, core), sample: 8 (over z, x).
Axes of the slice: x: 2, y: 2, z: 4, core: 2. Of those that a mesh axis runs over, the one named last changes fastest.
Arguments:
- centres: bfloat16 [1024, 8192], P(None, 'centre'), may hold values from -40 to 40
- pool: bfloat16 [1024, 8192], P('centre', 'sample'), may hold values from -40 to 40
- labels: int32 [8192], P('sample'), may hold values from 0 to 143
- picks: int32 [2, 4096], P(None, 'sample'), may hold values from 0 to 8191, as said below
- coefs: float32 [144, 8192], P(None, ('centre', 'sample')), may hold values from -192 to 256000
Outputs:
- new_coefs: float32 [144, 8192], P(None, ('centre', 'sample'))
Inputs may be any that keep to these rules, and one draw needn't show every extreme that they name: `picks`: entry b of a step's batch is a pool column in [(b // 512) * 1024, (b // 512 + 1) * 1024); entries may repeat.
All inputs are finite; a program needn't handle non-finite values.
Results may differ from a plain program's by a relative error of at most 0.00065.
Values may be sent and summed in bfloat16 or wider, within the bound.
A program may use at most 64 MiB of HBM per device.

v0:
```python
import functools
import math

import jax
import jax.numpy as jnp
from jax import lax
from jax.experimental import pallas as pl
from jax.experimental.pallas import tpu as pltpu
from jax.sharding import PartitionSpec as P

LOGIT_GAIN = 16.0
LENGTH_SCALE = 0.5
STEP_GAIN = 2048.0
EPS = 1e-06

GRAD_WIRE = jnp.bfloat16
LOGIT_WIRE = jnp.float32
MESH = pl.DeviceIdType.MESH
NT = (((1,), (1,)), ((), ()))


def kernel(
    n_c, n_s, logit_scale, rate,
    cen_hbm, pool_ref, labels_ref, picks_ref, coefs_ref, out_ref,
    cen, csq, feats, kern, labs, coefb, lsend, lrecv, resid, gsend, grecv, psend, precv, cur,
    cen_sem, send_sem, feat_sem, log_sem, res_sem, coef_sem, grad_sem,
):
    steps, batch = picks_ref.shape
    fd, pool_dev = pool_ref.shape
    classes, own = coefs_ref.shape
    width, cen_dev = cen.shape
    share = batch // n_c
    ny = n_c // 2
    tile = max(own, min(256, cen_dev))
    pieces = tile // own

    c = lax.axis_index("centre")
    s = lax.axis_index("sample")
    sib = c + 1 - 2 * lax.rem(c, 2)
    c_peers = [lax.rem(c + r, n_c) for r in range(1, n_c)]
    s_peers = [lax.rem(s + r, n_s) for r in range(1, n_s)]
    pair = s + 1 - 2 * lax.rem(s, 2)
    nz = n_s // 2
    order = sorted(range(1, nz), key=lambda q: -min(q, nz - q))

    barrier = pltpu.get_barrier_semaphore()
    for peer in c_peers:
        pl.semaphore_signal(barrier, inc=1, device_id={"centre": peer}, device_id_type=MESH)
    for peer in s_peers:
        pl.semaphore_signal(barrier, inc=1, device_id={"sample": peer}, device_id_type=MESH)

    load = pltpu.make_async_copy(cen_hbm, cen, cen_sem)
    load.start()
    started = []

    def send(src, dst, recv, axis, peer):
        copy = pltpu.make_async_remote_copy(
            src_ref=src, dst_ref=dst, send_sem=send_sem.at[len(started)], recv_sem=recv,
            device_id={axis: peer}, device_id_type=MESH,
        )
        copy.start()
        started.append(copy)
        return copy

    label_rows = jnp.broadcast_to(labels_ref[...].astype(jnp.float32), (16, pool_dev)).astype(jnp.bfloat16)

    def pick(t):
        chosen = picks_ref[t:t + 1, :] - s * pool_dev
        rows = lax.broadcasted_iota(jnp.int32, (pool_dev, batch), 0)
        hot = jnp.where(rows == chosen, -2.0, 0.0).astype(jnp.bfloat16)
        got = jnp.dot(pool_ref[...], hot, preferred_element_type=jnp.float32)
        feats[t, c] = got.T.astype(jnp.bfloat16)
        lab = -0.5 * jnp.dot(label_rows, hot, preferred_element_type=jnp.float32)
        for k in range(n_c):
            labs[t, k] = lab[0:8, k * share:(k + 1) * share]

    def send_feats(t):
        mine = feats.at[t, c]
        direct = []
        for q in range(1, ny):
            direct.append(send(mine, mine, feat_sem.at[t, q], "centre", lax.rem(c + 2 * q, n_c)))
        return [send(mine, mine, feat_sem.at[t, 0], "centre", sib)], direct

    def forward_feats(t, near, direct):
        for q, copy in enumerate(direct, 1):
            copy.wait_recv()
            slot = feats.at[t, lax.rem(c - 2 * q + n_c, n_c)]
            near.append(send(slot, slot, feat_sem.at[t, ny - 1 + q], "centre", sib))
        for copy in near:
            copy.wait_recv()

    def send_coefs(t):
        mine = coefb.at[t, s]
        direct = [
            (q, send(mine, mine, coef_sem.at[t, q], "sample", lax.rem(s + 2 * q, n_s)))
            for q in order
        ]
        return [send(mine, mine, coef_sem.at[t, 0], "sample", pair)], direct

    def forward_coefs(t, near, direct):
        for q, copy in direct:
            copy.wait_recv()
            slot = coefb.at[t, lax.rem(s - 2 * q + n_s, n_s)]
            near.append(send(slot, slot, coef_sem.at[t, nz - 1 + q], "sample", pair))

    cur[...] = coefs_ref[...]
    coefb[0, s] = coefs_ref[...].astype(jnp.bfloat16)
    pl.semaphore_wait(barrier, n_c - 1 + n_s - 1)
    coef_near, coef_direct = send_coefs(0)
    pick(0)
    moves = [send_feats(0)]
    pick(1)
    moves.append(send_feats(1))

    load.wait()

    def square(j, _):
        cols = pl.ds(pl.multiple_of(j * tile, tile), tile)
        block = cen[:, cols].astype(jnp.float32)
        csq[:, cols] = jnp.sum(block * block, axis=0, keepdims=True)
        return 0

    lax.fori_loop(0, cen_dev // tile, square, 0)

    bend = (1.0 / (LENGTH_SCALE * math.log(2.0))) ** 2

    def laplace(t):
        parts = [feats[t, k] for k in range(n_c)]
        ssq = sum(
            jnp.sum(jnp.square(p.astype(jnp.float32)), axis=1, keepdims=True) for p in parts
        ) * 0.25
        if fd % 128 == 0:
            parts = [jnp.concatenate(parts, axis=1)]
        deep = width // len(parts)

        def body(j, _):
            cols = pl.ds(pl.multiple_of(j * tile, tile), tile)
            cross = sum(
                jnp.dot(p, cen[k * deep:(k + 1) * deep, cols], preferred_element_type=jnp.float32)
                for k, p in enumerate(parts)
            )
            arg = ((ssq + csq[:, cols]) + cross) * (bend / width) + bend * EPS
            arg = jnp.maximum(arg, 1e-30)
            value = jnp.exp2(-(arg * lax.rsqrt(arg)))
            for k in range(pieces):
                kern[t, j * pieces + k] = value[:, k * own:(k + 1) * own].astype(jnp.bfloat16)
            return 0

        lax.fori_loop(0, cen_dev // tile, body, 0)

    def residual(t):
        part = sum(
            lax.dot_general(coefb[t, j], kern[t, j], NT, preferred_element_type=jnp.float32)
            for j in range(n_s)
        )
        for k in range(n_c):
            lsend[t, k] = part[:, k * share:(k + 1) * share].astype(LOGIT_WIRE)
        copies = [
            send(lsend.at[t, peer], lrecv.at[t, r], log_sem.at[t, r], "centre", peer)
            for r, peer in enumerate(c_peers)
        ]
        if t + 1 < steps:
            forward_feats(t + 1, *moves[t + 1])
        total = lsend[t, c].astype(jnp.float32)
        for r, copy in enumerate(copies):
            copy.wait_recv()
            total = total + lrecv[t, r].astype(jnp.float32)
        logits = total * logit_scale
        expo = jnp.exp(logits - jnp.max(logits, axis=0, keepdims=True))
        probs = expo / jnp.sum(expo, axis=0, keepdims=True)
        ids = lax.broadcasted_iota(jnp.int32, (classes, share), 0).astype(jnp.float32)
        hot = jnp.where(ids == labs[t, c][0:1, :], 1.0, 0.0)
        resid[t, c] = (probs - hot).astype(jnp.bfloat16)
        mine = resid.at[t, c]
        copies = [
            send(mine, mine, res_sem.at[t, r], "centre", peer) for r, peer in enumerate(c_peers)
        ]
        for copy in copies:
            copy.wait_recv()

    def gradient(t):
        if share % 128 == 0:
            whole = jnp.concatenate([resid[t, k] for k in range(n_c)], axis=1)

            def grad(j):
                return jnp.dot(whole, kern[t, j], preferred_element_type=jnp.float32)
        else:
            def grad(j):
                return sum(
                    jnp.dot(resid[t, k], kern[t, j, k * share:(k + 1) * share, :],
                            preferred_element_type=jnp.float32)
                    for k in range(n_c)
                )
        def put(i, value, peer):
            gsend[t, i] = value.astype(GRAD_WIRE)
            return send(gsend.at[t, i], grecv.at[t, i], grad_sem.at[t, i], "sample", peer)

        far = [lax.rem(start + 2 * q, n_s) for q in order for start in (s, pair)]
        copies = [put(i, grad(peer), peer) for i, peer in enumerate(far)]
        psend[t] = grad(pair)
        last = send(psend.at[t], precv.at[t], grad_sem.at[t, n_s - 2], "sample", pair)
        return grad(s), last, copies

    forward_coefs(0, coef_near, coef_direct[:2])
    forward_feats(0, *moves[0])
    forward_coefs(0, coef_near, coef_direct[2:])
    laplace(0)
    for t in range(steps):
        for copy in coef_near:
            copy.wait_recv()
        residual(t)
        total, last, copies = gradient(t)
        if t + 1 < steps:
            laplace(t + 1)
        last.wait_recv()
        total = total + precv[t]
        for r, copy in enumerate(copies):
            copy.wait_recv()
            total = total + grecv[t, r].astype(jnp.float32)
        fresh = cur[...] - rate * total
        if t + 1 < steps:
            cur[...] = fresh
            coefb[t + 1, s] = fresh.astype(jnp.bfloat16)
            coef_near, coef_direct = send_coefs(t + 1)
            forward_coefs(t + 1, coef_near, coef_direct)
        else:
            out_ref[...] = fresh
    for copy in started:
        copy.wait_send()


def on_device(n_c, n_s, centres, pool, labels, picks, coefs):
    width, cen_dev = centres.shape
    fd, pool_dev = pool.shape
    steps, batch = picks.shape
    classes, own = coefs.shape
    share = batch // n_c
    bf16, f32 = jnp.bfloat16, jnp.float32
    body = functools.partial(
        kernel, n_c, n_s, LOGIT_GAIN / (cen_dev * n_c), STEP_GAIN * LOGIT_GAIN / (batch * n_s)
    )
    vmem = pl.BlockSpec(memory_space=pltpu.VMEM)
    return pl.pallas_call(
        body,
        out_shape=jax.ShapeDtypeStruct((classes, own), f32),
        in_specs=[pl.BlockSpec(memory_space=pl.ANY)] + [vmem] * 4,
        out_specs=vmem,
        scratch_shapes=[
            pltpu.VMEM((width, cen_dev), bf16),
            pltpu.VMEM((1, cen_dev), f32),
            pltpu.VMEM((steps, n_c, batch, fd), bf16),
            pltpu.VMEM((steps, n_s, batch, own), bf16),
            pltpu.VMEM((steps, n_c, 8, share), f32),
            pltpu.VMEM((steps, n_s, classes, own), bf16),
            pltpu.VMEM((steps, n_c, classes, share), LOGIT_WIRE),
            pltpu.VMEM((steps, n_c - 1, classes, share), LOGIT_WIRE),
            pltpu.VMEM((steps, n_c, classes, share), bf16),
            pltpu.VMEM((steps, n_s - 2, classes, own), GRAD_WIRE),
            pltpu.VMEM((steps, n_s - 2, classes, own), GRAD_WIRE),
            pltpu.VMEM((steps, classes, own), f32),
            pltpu.VMEM((steps, classes, own), f32),
            pltpu.VMEM((classes, own), f32),
            pltpu.SemaphoreType.DMA,
            pltpu.SemaphoreType.DMA((steps * (3 * (n_c - 1) + 2 * (n_s - 1)),)),
            pltpu.SemaphoreType.DMA((steps, n_c - 1)),
            pltpu.SemaphoreType.DMA((steps, n_c - 1)),
            pltpu.SemaphoreType.DMA((steps, n_c - 1)),
            pltpu.SemaphoreType.DMA((steps, n_s - 1)),
            pltpu.SemaphoreType.DMA((steps, n_s - 1)),
        ],
        compiler_params=pltpu.CompilerParams(
            collective_id=0, has_side_effects=True, vmem_limit_bytes=60 * 1024 * 1024
        ),
    )(centres, pool, labels.reshape(1, pool_dev), picks, coefs)


def solution(mesh):
    placed = (
        P(None, "centre"),
        P("centre", "sample"),
        P("sample"),
        P(None, "sample"),
        P(None, ("centre", "sample")),
    )
    return jax.shard_map(
        functools.partial(on_device, mesh.shape["centre"], mesh.shape["sample"]),
        mesh=mesh,
        in_specs=placed,
        out_specs=P(None, ("centre", "sample")),
        check_vma=False,
    )
```

profile of v0, /device:TPU:0, one launch (start us, length us, event | category | flops | bytes accessed | tf_op | source)
XLA Modules:
  0.0 80.8 jit_solution(12516927235260679904)
XLA Ops:
  0.0 79.2 %shard_map.55 = f32[144,256]{1,0:T(8,128)} custom-call(bf16[1024,2048]{1,0:T(8,128)(2,1)} %cen_hbm.1, bf16[256,1024]{1,0:T(8,128)(2,1)} %pool_ref.1, s32[1,1024]{1,0:T(1,128)} %bitcast.1, s32[2,512]{1,0:T(2,128)} %picks_ref.1, f32[144,256]{1,0:T(8,128)} %coefs_ref.1), custom_call_target="tpu_custom_call" | custom-call | tf_op jit(solution)/shard_map/pallas_call | solution.py:243
  79.2 1.6 %copy.7 = f32[144,256]{1,0:T(8,128)} copy(f32[144,256]{1,0:T(8,128)} %shard_map.55) | data formatting | bytes 294912
where the time goes:
time: 81.5 us; the launch traced here: 80.8 us
  Pallas kernels  79.2 us (97%)
  local copies, waits for them, and re-layouts  1.58 us (2%)
    pallas_call x1, Pallas kernels, on_device(): pl.pallas_call(body, out_shape=jax.ShapeDtypeStruct((classes, own), f32),...  79.2 us

commit v1 on v0

--- a/solution.py
+++ b/solution.py
@@ -229,7 +229,474 @@
         copy.wait_send()
 
 
-def on_device(n_c, n_s, centres, pool, labels, picks, coefs):
+CHUNKS = 2
+PIECES = 3
+LOG_STEPS = 520.0
+LOG_LOW = 50.0
+
+
+def encode(value):
+    size = jnp.maximum(jnp.abs(value), 2.0 ** -LOG_LOW)
+    code = jnp.round((jnp.log(size) * (1.0 / math.log(2.0)) + LOG_LOW) * LOG_STEPS)
+    return jnp.where(value < 0.0, -code, code).astype(jnp.int16)
+
+
+def decode(code):
+    number = code.astype(jnp.float32)
+    size = jnp.exp2(jnp.abs(number) * (1.0 / LOG_STEPS) - LOG_LOW)
+    return jnp.where(number < 0.0, -size, jnp.where(number > 0.0, size, 0.0))
+
+
+def line_kernel(
+    logit_scale, rate,
+    cen_hbm, pool_hbm, labels_hbm, picks_hbm, coefs_hbm, out_ref,
+    cen, pool_ref, labels_ref, picks_ref, cur,
+    csq, feats, kern, labs, coefb, lpart, lrecv, lsum, ysum, resid, gown,
+    xsend, xrecv, asend, arecv, bsend, brecv,
+    load_sem, send_sem, feat_sem, log_sem, red_x, red_a, red_b, coef_x, coef_a, coef_b,
+):
+    steps, batch = picks_ref.shape
+    fd, pool_dev = pool_ref.shape
+    classes, own = cur.shape
+    width, cen_dev = cen.shape
+    blocks = cen_dev // own
+    rows_n = batch // CHUNKS
+    half = rows_n // 2
+    piece = classes // PIECES
+    tile = 2 * own
+
+    c = lax.axis_index("centre")
+    s = lax.axis_index("sample")
+    y, k = lax.div(c, 2), lax.rem(c, 2)
+    z, x = lax.div(s, 2), lax.rem(s, 2)
+    side = lax.div(z, 2)
+    inner = lax.rem(z + side, 2)
+    is_inner = inner == 1
+    is_outer = inner == 0
+    SO, SI, OI, OO = 3 * side, 1 + side, 2 - side, 3 - 3 * side
+    sib_c = c + 1 - 2 * k
+    far_c = (1 - y) * 2 + k
+    far_sib_c = (1 - y) * 2 + 1 - k
+    sib = {"centre": sib_c}
+    far = {"centre": far_c}
+    xp = {"sample": z * 2 + 1 - x}
+    za = {"sample": (z + 1 - 2 * lax.rem(z, 2)) * 2 + x}
+    zb = {"sample": (3 - z) * 2 + x}
+
+    barrier = pltpu.get_barrier_semaphore()
+    for peer in (sib, far, xp, za, zb):
+        pl.semaphore_signal(barrier, inc=1, device_id=peer, device_id_type=MESH)
+
+    loads = [
+        pltpu.make_async_copy(src, dst, load_sem.at[i])
+        for i, (src, dst) in enumerate(
+            [(picks_hbm, picks_ref), (pool_hbm, pool_ref), (labels_hbm, labels_ref), (coefs_hbm, cur), (cen_hbm, cen)]
+        )
+    ]
+    for copy in loads:
+        copy.start()
+
+    used = []
+
+    def make(src, dst, recv, peer):
+        used.append(pltpu.make_async_remote_copy(
+            src_ref=src, dst_ref=dst, send_sem=send_sem.at[len(used)], recv_sem=recv,
+            device_id=peer, device_id_type=MESH,
+        ))
+        return used[-1]
+
+    def rows_of(i):
+        return slice(i * rows_n, (i + 1) * rows_n)
+
+    def piece_of(h):
+        return slice(h * piece, (h + 1) * piece)
+
+    everyone, outers, inners = [], [], []
+
+    def plain(*args):
+        copy = make(*args)
+        everyone.append(copy)
+        return copy
+
+    feat_far = [[plain(feats.at[t, c, rows_of(i)], feats.at[t, c, rows_of(i)], feat_sem.at[t, 0, i], far)
+                 for i in range(CHUNKS)] for t in range(steps)]
+    feat_sib = [[plain(feats.at[t, c, rows_of(i)], feats.at[t, c, rows_of(i)], feat_sem.at[t, 1, i], sib)
+                 for i in range(CHUNKS)] for t in range(steps)]
+    feat_fwd = [[plain(feats.at[t, far_c, rows_of(i)], feats.at[t, far_c, rows_of(i)], feat_sem.at[t, 2, i], sib)
+                 for i in range(CHUNKS)] for t in range(steps)]
+    log_sib = [[plain(lpart.at[t, i, 1 - k], lrecv.at[t, i], log_sem.at[t, 0, i], sib)
+                for i in range(CHUNKS)] for t in range(steps)]
+    log_far = [[plain(lsum.at[t, i], ysum.at[t, i], log_sem.at[t, 1, i], far)
+                for i in range(CHUNKS)] for t in range(steps)]
+    res_sib = [[plain(resid.at[t, i, k], resid.at[t, i, k], log_sem.at[t, 2, i], sib)
+                for i in range(CHUNKS)] for t in range(steps)]
+    sum_x = [[[plain(xsend.at[t, p, piece_of(h)], xrecv.at[t, p, piece_of(h)], red_x.at[t, p, h], xp)
+               for h in range(PIECES)] for p in range(4)] for t in range(steps)]
+
+    def group(store, *args):
+        copy = make(*args)
+        store.append(copy)
+        return copy
+
+    sum_a = [[[make(asend.at[t, p, piece_of(h)], arecv.at[t, p, piece_of(h)], red_a.at[t, p, h], za)
+               for h in range(PIECES)] for p in range(3)] for t in range(steps)]
+    sum_b = [[[make(bsend.at[t, p, piece_of(h)], brecv.at[t, p, piece_of(h)], red_b.at[t, p, h], zb)
+               for h in range(PIECES)] for p in range(2)] for t in range(steps)]
+    for t in range(steps):
+        for h in range(PIECES):
+            outers.extend([sum_a[t][p][h] for p in range(3)])
+            inners.extend([sum_a[t][0][h], sum_b[t][0][h], sum_b[t][1][h]])
+
+    names = (SO, SI, OI, OO)
+
+    def coef_copy(t, name, h, sem, peer):
+        slot = coefb.at[t, name * 2 + x, piece_of(h)]
+        return make(slot, slot, sem, peer)
+
+    put_x = [[[coef_copy(t, names[n], h, coef_x.at[t, n, h], xp) for h in range(PIECES)] for n in range(4)]
+             for t in range(steps)]
+    out_a = [[coef_copy(t, SO, h, coef_a.at[t, 0, h], za) for h in range(PIECES)] for t in range(steps)]
+    in_a = [[[coef_copy(t, names[1 + n], h, coef_a.at[t, n, h], za) for h in range(PIECES)] for n in range(3)]
+            for t in range(steps)]
+    in_b = [[[coef_copy(t, (SI, SO)[n], h, coef_b.at[t, n, h], zb) for h in range(PIECES)] for n in range(2)]
+            for t in range(steps)]
+    for t in range(steps):
+        for h in range(PIECES):
+            everyone.extend([put_x[t][n][h] for n in range(4)])
+            outers.append(out_a[t][h])
+            inners.extend([in_a[t][n][h] for n in range(3)] + [in_b[t][n][h] for n in range(2)])
+
+    def pick(t):
+        chosen = picks_ref[t:t + 1, :] - s * pool_dev
+        rows = lax.broadcasted_iota(jnp.int32, (pool_dev, batch), 0)
+        hot = jnp.where(rows == chosen, -2.0, 0.0).astype(jnp.bfloat16)
+        got = jnp.dot(pool_ref[...], hot, preferred_element_type=jnp.float32)
+        feats[t, c] = got.T.astype(jnp.bfloat16)
+        return hot
+
+    def pick_labels(t, hot):
+        label_rows = jnp.broadcast_to(labels_ref[...].astype(jnp.float32), (16, pool_dev)).astype(jnp.bfloat16)
+        lab = -0.5 * jnp.dot(label_rows, hot, preferred_element_type=jnp.float32)
+        for n in range(2 * CHUNKS):
+            labs[t, n] = lab[0:8, n * half:(n + 1) * half]
+
+    bend = (1.0 / (LENGTH_SCALE * math.log(2.0))) ** 2
+
+    def laplace(t, i, first, last):
+        rows = rows_of(i)
+        ssq = sum(
+            jnp.sum(jnp.square(feats[t, q, rows].astype(jnp.float32)), axis=1, keepdims=True) for q in range(4)
+        ) * 0.25
+
+        def body(j, _):
+            cols = pl.ds(pl.multiple_of(j * tile, tile), tile)
+            lhs = jnp.concatenate([feats[t, q, rows] for q in range(4)], axis=1)
+            cross = jnp.dot(lhs, cen[:, cols], preferred_element_type=jnp.float32)
+            arg = ((ssq + csq[:, cols]) + cross) * (bend / width) + bend * EPS
+            arg = jnp.maximum(arg, 1e-30)
+            value = jnp.exp2(-(arg * lax.rsqrt(arg)))
+            for q in range(2):
+                kern[t, j * 2 + q, rows] = value[:, q * own:(q + 1) * own].astype(jnp.bfloat16)
+            return 0
+
+        lax.fori_loop(first, last, body, 0)
+
+    tiles = cen_dev // tile
+
+    def logits(t, i):
+        part = sum(
+            lax.dot_general(coefb[t, j], kern[t, j, rows_of(i)], NT, preferred_element_type=jnp.float32)
+            for j in range(blocks)
+        )
+        for h in range(2):
+            lpart[t, i, h] = part[:, h * half:(h + 1) * half]
+        log_sib[t][i].start()
+
+    def chip_sum(t, i):
+        log_sib[t][i].wait_recv()
+        lsum[t, i] = lpart[t, i, k] + lrecv[t, i]
+        log_far[t][i].start()
+
+    def residual(t, i):
+        log_far[t][i].wait_recv()
+        value = (lsum[t, i] + ysum[t, i]) * logit_scale
+        expo = jnp.exp(value - jnp.max(value, axis=0, keepdims=True))
+        probs = expo / jnp.sum(expo, axis=0, keepdims=True)
+        ids = lax.broadcasted_iota(jnp.int32, (classes, half), 0).astype(jnp.float32)
+        hot = jnp.where(ids == labs[t, 2 * i + k][0:1, :], 1.0, 0.0)
+        resid[t, i, k] = (probs - hot).astype(jnp.bfloat16)
+        res_sib[t][i].start()
+
+    def swap(now, later):
+        return jnp.where(is_inner, later, now)
+
+    order = (OO, swap(OI, SO), swap(SI, OI), swap(SO, SI))
+
+    def gradient(t):
+        for i in range(CHUNKS):
+            res_sib[t][i].wait_recv()
+        whole = jnp.concatenate([resid[t, i, h] for i in range(CHUNKS) for h in range(2)], axis=1)
+
+        def grad(zd, xd):
+            return jnp.dot(whole, kern[t, zd * 2 + xd], preferred_element_type=jnp.float32)
+
+        for p in range(4):
+            xsend[t, p] = encode(grad(order[p], 1 - x))
+            for h in range(PIECES):
+                sum_x[t][p][h].start()
+        for p in range(4):
+            gown[p] = grad(order[p], x)
+
+    def chain(t, p):
+        def add_x(h):
+            sum_x[t][p][h].wait_recv()
+            return gown[p, piece_of(h)] + decode(xrecv[t, p, piece_of(h)])
+
+        @pl.when(is_outer)
+        def _():
+            for h in range(PIECES):
+                value = add_x(h)
+                if p < 3:
+                    asend[t, p, piece_of(h)] = encode(value)
+                    sum_a[t][p][h].start()
+                else:
+                    sum_a[t][0][h].wait_recv()
+                    gown[3, piece_of(h)] = value + decode(arecv[t, 0, piece_of(h)])
+
+        @pl.when(is_inner)
+        def _():
+            for h in range(PIECES):
+                value = add_x(h)
+                rows = piece_of(h)
+                if p == 0:
+                    sum_a[t][0][h].wait_recv()
+                    bsend[t, 0, rows] = encode(value + decode(arecv[t, 0, rows]))
+                    sum_b[t][0][h].start()
+                elif p == 1:
+                    sum_b[t][0][h].wait_recv()
+                    asend[t, 0, rows] = encode(value + decode(brecv[t, 0, rows]))
+                    sum_a[t][0][h].start()
+                elif p == 2:
+                    sum_a[t][1][h].wait_recv()
+                    bsend[t, 1, rows] = encode(value + decode(arecv[t, 1, rows]))
+                    sum_b[t][1][h].start()
+                else:
+                    sum_a[t][2][h].wait_recv()
+                    sum_b[t][1][h].wait_recv()
+                    gown[3, rows] = value + decode(arecv[t, 2, rows]) + decode(brecv[t, 1, rows])
+
+    def share_own(t):
+        @pl.when(is_outer)
+        def _():
+            for h in range(PIECES):
+                out_a[t][h].start()
+                put_x[t][0][h].start()
+
+        @pl.when(is_inner)
+        def _():
+            for h in range(PIECES):
+                in_b[t][0][h].start()
+                in_a[t][0][h].start()
+                put_x[t][1][h].start()
+
+    def share_hop(t, hop):
+        @pl.when(is_outer)
+        def _():
+            for h in range(PIECES):
+                in_a[t][hop][h].wait_recv()
+                put_x[t][1 + hop][h].start()
+
+        @pl.when(is_inner)
+        def _():
+            for h in range(PIECES):
+                if hop == 0:
+                    out_a[t][h].wait_recv()
+                    in_b[t][1][h].start()
+                    in_b[t][0][h].wait_recv()
+                    in_a[t][1][h].start()
+                    put_x[t][0][h].start()
+                    put_x[t][2][h].start()
+                elif hop == 1:
+                    in_b[t][1][h].wait_recv()
+                    in_a[t][2][h].start()
+                    put_x[t][3][h].start()
+
+    def share_end(t):
+        for n in range(4):
+            for h in range(PIECES):
+                put_x[t][n][h].wait_recv()
+
+    loads[0].wait()
+    loads[1].wait()
+    hots = pick(0)
+    pl.semaphore_wait(barrier, 5)
+    for i in range(CHUNKS):
+        feat_far[0][i].start()
+        feat_sib[0][i].start()
+    loads[3].wait()
+    coefb[0, s] = cur[...].astype(jnp.bfloat16)
+    share_own(0)
+    loads[2].wait()
+    pick_labels(0, hots)
+    pick_labels(1, pick(1))
+    loads[4].wait()
+
+    def square(j, _):
+        cols = pl.ds(pl.multiple_of(j * own, own), own)
+        block = cen[:, cols].astype(jnp.float32)
+        csq[:, cols] = jnp.sum(block * block, axis=0, keepdims=True)
+        return 0
+
+    lax.fori_loop(0, cen_dev // own, square, 0)
+
+    share_hop(0, 0)
+    feat_far[0][0].wait_recv()
+    feat_fwd[0][0].start()
+    share_hop(0, 1)
+    feat_sib[0][0].wait_recv()
+    feat_fwd[0][0].wait_recv()
+    laplace(0, 0, 0, tiles // 2)
+    share_hop(0, 2)
+    laplace(0, 0, tiles // 2, tiles)
+    feat_far[0][1].wait_recv()
+    feat_fwd[0][1].start()
+    share_end(0)
+    logits(0, 0)
+    feat_sib[0][1].wait_recv()
+    feat_fwd[0][1].wait_recv()
+    laplace(0, 1, 0, tiles // 2)
+    chip_sum(0, 0)
+    laplace(0, 1, tiles // 2, tiles)
+    logits(0, 1)
+    residual(0, 0)
+    chip_sum(0, 1)
+    for i in range(CHUNKS):
+        feat_far[1][i].start()
+        feat_sib[1][i].start()
+    residual(0, 1)
+
+    gradient(0)
+    chain(0, 0)
+    feat_far[1][0].wait_recv()
+    feat_fwd[1][0].start()
+    chain(0, 1)
+    feat_sib[1][0].wait_recv()
+    feat_fwd[1][0].wait_recv()
+    laplace(1, 0, 0, 1)
+    chain(0, 2)
+    laplace(1, 0, 1, 2)
+    chain(0, 3)
+    fresh = cur[...] - rate * gown[3]
+    cur[...] = fresh
+    coefb[1, s] = fresh.astype(jnp.bfloat16)
+    share_own(1)
+    feat_far[1][1].wait_recv()
+    feat_fwd[1][1].start()
+    laplace(1, 0, 2, tiles)
+    feat_sib[1][1].wait_recv()
+    feat_fwd[1][1].wait_recv()
+    share_hop(1, 0)
+    laplace(1, 1, 0, 1)
+    share_hop(1, 1)
+    laplace(1, 1, 1, 2)
+    share_hop(1, 2)
+    laplace(1, 1, 2, tiles)
+    share_end(1)
+    for i in range(CHUNKS):
+        logits(1, i)
+    for i in range(CHUNKS):
+        chip_sum(1, i)
+    for i in range(CHUNKS):
+        residual(1, i)
+    gradient(1)
+    for p in range(4):
+        chain(1, p)
+    out_ref[...] = cur[...] - rate * gown[3]
+
+    for copy in everyone:
+        copy.wait_send()
+
+    @pl.when(is_outer)
+    def _():
+        for copy in outers:
+            copy.wait_send()
+
+    @pl.when(is_inner)
+    def _():
+        for copy in inners:
+            copy.wait_send()
+
+
+def line_device(n_c, n_s, centres, pool, labels, picks, coefs):
+    width, cen_dev = centres.shape
+    fd, pool_dev = pool.shape
+    steps, batch = picks.shape
+    classes, own = coefs.shape
+    half = batch // CHUNKS // 2
+    bf16, f32 = jnp.bfloat16, jnp.float32
+    anyspace = pl.BlockSpec(memory_space=pl.ANY)
+    dma = pltpu.SemaphoreType.DMA
+    copies = steps * (6 * CHUNKS + (4 + 3 + 2 + 4 + 1 + 3 + 2) * PIECES)
+    return pl.pallas_call(
+        functools.partial(
+            line_kernel, LOGIT_GAIN / (cen_dev * n_c), STEP_GAIN * LOGIT_GAIN / (batch * n_s)
+        ),
+        out_shape=jax.ShapeDtypeStruct((classes, own), f32),
+        in_specs=[anyspace] * 5,
+        out_specs=pl.BlockSpec(memory_space=pltpu.VMEM),
+        scratch_shapes=[
+            pltpu.VMEM((width, cen_dev), bf16),
+            pltpu.VMEM((fd, pool_dev), bf16),
+            pltpu.VMEM((1, pool_dev), jnp.int32),
+            pltpu.VMEM((steps, batch), jnp.int32),
+            pltpu.VMEM((classes, own), f32),
+            pltpu.VMEM((1, cen_dev), f32),
+            pltpu.VMEM((steps, n_c, batch, fd), bf16),
+            pltpu.VMEM((steps, n_s, batch, own), bf16),
+            pltpu.VMEM((steps, 2 * CHUNKS, 8, half), f32),
+            pltpu.VMEM((steps, n_s, classes, own), bf16),
+            pltpu.VMEM((steps, CHUNKS, 2, classes, half), f32),
+            pltpu.VMEM((steps, CHUNKS, classes, half), f32),
+            pltpu.VMEM((steps, CHUNKS, classes, half), f32),
+            pltpu.VMEM((steps, CHUNKS, classes, half), f32),
+            pltpu.VMEM((steps, CHUNKS, 2, classes, half), bf16),
+            pltpu.VMEM((4, classes, own), f32),
+            pltpu.VMEM((steps, 4, classes, own), jnp.int16),
+            pltpu.VMEM((steps, 4, classes, own), jnp.int16),
+            pltpu.VMEM((steps, 3, classes, own), jnp.int16),
+            pltpu.VMEM((steps, 3, classes, own), jnp.int16),
+            pltpu.VMEM((steps, 2, classes, own), jnp.int16),
+            pltpu.VMEM((steps, 2, classes, own), jnp.int16),
+            dma((5,)),
+            dma((copies,)),
+            dma((steps, 3, CHUNKS)),
+            dma((steps, 3, CHUNKS)),
+            dma((steps, 4, PIECES)),
+            dma((steps, 3, PIECES)),
+            dma((steps, 2, PIECES)),
+            dma((steps, 4, PIECES)),
+            dma((steps, 3, PIECES)),
+            dma((steps, 2, PIECES)),
+        ],
+        compiler_params=pltpu.CompilerParams(
+            collective_id=0, has_side_effects=True, vmem_limit_bytes=60 * 1024 * 1024
+        ),
+    )(centres, pool, labels.reshape(1, pool_dev), picks, coefs)
+
+
+def suits_line(mesh, centres, pool, picks, coefs):
+    n_c, n_s = mesh.shape["centre"], mesh.shape["sample"]
+    own, batch, fd = coefs.shape[1], picks.shape[1], pool.shape[0]
+    return (
+        n_c == 4 and n_s == 8 and own % 128 == 0 and fd % 128 == 0 and picks.shape[0] == 2
+        and batch % (256 * CHUNKS) == 0 and coefs.shape[0] % (16 * PIECES) == 0 and batch * n_s <= 4096
+    )
+
+
+def on_device(mesh, centres, pool, labels, picks, coefs):
+    n_c, n_s = mesh.shape["centre"], mesh.shape["sample"]
+    if suits_line(mesh, centres, pool, picks, coefs):
+        return line_device(n_c, n_s, centres, pool, labels, picks, coefs)
     width, cen_dev = centres.shape
     fd, pool_dev = pool.shape
     steps, batch = picks.shape
@@ -283,7 +750,7 @@
         P(None, ("centre", "sample")),
     )
     return jax.shard_map(
-        functools.partial(on_device, mesh.shape["centre"], mesh.shape["sample"]),
+        functools.partial(on_device, mesh),
         mesh=mesh,
         in_specs=placed,
         out_specs=P(None, ("centre", "sample")),

time: 81.5 us -> 78.6 us (0.964)
  Pallas kernels: 79.2 us -> 76.8 us
    pallas_call x1, Pallas kernels: 79.2 us -> 76.8 us  [line_device(): pl.pallas_call(functools.partial(line_kernel, LOGIT_GAIN / (cen_dev * n_c...]
where the time goes in v1:
time: 78.6 us; the launch traced here: 78.4 us
  Pallas kernels  76.8 us (98%)
  local copies, waits for them, and re-layouts  1.58 us (2%)
    pallas_call x1, Pallas kernels, line_device(): pl.pallas_call(functools.partial(line_kernel, LOGIT_GAIN / (cen_dev * n_c...  76.8 us
    unnamed x1, local copies, waits for them, and re-layouts  1.58 us

profile of v1, /device:TPU:0, one launch (start us, length us, event | category | flops | bytes accessed | tf_op | source)
XLA Modules:
  0.0 78.4 jit_solution(3147635386773049906)
XLA Ops:
  0.0 76.8 %shard_map.55 = f32[144,256]{1,0:T(8,128)} custom-call(bf16[1024,2048]{1,0:T(8,128)(2,1)} %cen_hbm.1, bf16[256,1024]{1,0:T(8,128)(2,1)} %pool_hbm.1, s32[1,1024]{1,0:T(1,128)} %bitcast.1, s32[2,512]{1,0:T(2,128)} %picks_hbm.1, f32[144,256]{1,0:T(8,128)} %coefs_hbm.1), custom_call_target="tpu_custom_call" | custom-call | tf_op jit(solution)/shard_map/pallas_call | solution.py:640
  76.8 1.6 %copy.7 = f32[144,256]{1,0:T(8,128)} copy(f32[144,256]{1,0:T(8,128)} %shard_map.55) | data formatting | bytes 294912

commit v2 on v0

--- a/solution.py
+++ b/solution.py
@@ -229,7 +229,412 @@
         copy.wait_send()
 
 
-def on_device(n_c, n_s, centres, pool, labels, picks, coefs):
+CHUNKS = 2
+PIECES = 3
+LOG_STEPS = 520.0
+LOG_LOW = 50.0
+
+
+def encode(value):
+    size = jnp.maximum(jnp.abs(value), 2.0 ** -LOG_LOW)
+    code = jnp.round((jnp.log(size) * (1.0 / math.log(2.0)) + LOG_LOW) * LOG_STEPS)
+    return jnp.where(value < 0.0, -code, code).astype(jnp.int16)
+
+
+def decode(code):
+    number = code.astype(jnp.float32)
+    size = jnp.exp2(jnp.abs(number) * (1.0 / LOG_STEPS) - LOG_LOW)
+    return jnp.where(number < 0.0, -size, jnp.where(number > 0.0, size, 0.0))
+
+
+def line_kernel(
+    logit_scale, rate,
+    cen_hbm, pool_hbm, labels_hbm, picks_hbm, coefs_hbm, out_ref,
+    cen, pool_ref, labels_ref, picks_ref, cur,
+    csq, feats, kern, labs, coefb, lacc, lpart, lrecv, lsum, ysum, resid, gown,
+    near_out, near_in, cross_out, cross_in,
+    load_sem, send_sem, feat_sem, log_sem, near_sem, cross_sem, mine_sem, over_sem, pass_sem,
+):
+    steps, batch = picks_ref.shape
+    fd, pool_dev = pool_ref.shape
+    classes, own = cur.shape
+    width, cen_dev = cen.shape
+    rows_n = batch // CHUNKS
+    half = rows_n // 2
+    piece = classes // PIECES
+    tile = 2 * own
+    tiles = cen_dev // tile
+
+    c = lax.axis_index("centre")
+    s = lax.axis_index("sample")
+    y, k = lax.div(c, 2), lax.rem(c, 2)
+    z, x = lax.div(s, 2), lax.rem(s, 2)
+    z_near = z + 1 - 2 * lax.rem(z, 2)
+    z_over = lax.rem(z + 2, 4)
+    z_both = lax.rem(z_near + 2, 4)
+    far_c = (1 - y) * 2 + k
+    sib = {"centre": c + 1 - 2 * k}
+    far = {"centre": far_c}
+    over = {"sample": z_over * 2 + x}
+    quad = [z * 2 + 1 - x, z_near * 2 + x, z_near * 2 + 1 - x]
+    across = [z_over * 2 + 1 - x, z_both * 2 + x, z_both * 2 + 1 - x]
+    near = [{"sample": q} for q in quad]
+
+    barrier = pltpu.get_barrier_semaphore()
+    for peer in [sib, far, over] + near:
+        pl.semaphore_signal(barrier, inc=1, device_id=peer, device_id_type=MESH)
+
+    loads = [
+        pltpu.make_async_copy(src, dst, load_sem.at[i])
+        for i, (src, dst) in enumerate(
+            [(picks_hbm, picks_ref), (pool_hbm, pool_ref), (labels_hbm, labels_ref), (coefs_hbm, cur), (cen_hbm, cen)]
+        )
+    ]
+    for i in (3, 0, 1, 2, 4):
+        loads[i].start()
+
+    def make(kind, t, src, dst, recv, peer):
+        return pltpu.make_async_remote_copy(
+            src_ref=src, dst_ref=dst, send_sem=send_sem.at[kind, t], recv_sem=recv,
+            device_id=peer, device_id_type=MESH,
+        )
+
+    def rows_of(i):
+        return slice(i * rows_n, (i + 1) * rows_n)
+
+    def piece_of(h):
+        return slice(h * piece, (h + 1) * piece)
+
+    def feat_copy(t, i, owner, n, peer):
+        slot = feats.at[t, owner, rows_of(i)]
+        return make(0, t, slot, slot, feat_sem.at[t, n, i], peer)
+
+    def feat_far(t, i):
+        return feat_copy(t, i, c, 0, far)
+
+    def feat_sib(t, i):
+        return feat_copy(t, i, c, 1, sib)
+
+    def feat_fwd(t, i):
+        return feat_copy(t, i, far_c, 2, sib)
+
+    def log_sib(t, i):
+        return make(1, t, lpart.at[t, i, 1 - k], lrecv.at[t, i], log_sem.at[0, t, i], sib)
+
+    def log_far(t, i):
+        return make(1, t, lsum.at[t, i], ysum.at[t, i], log_sem.at[1, t, i], far)
+
+    def res_sib(t, i):
+        return make(2, t, resid.at[t, i, k], resid.at[t, i, k], log_sem.at[2, t, i], sib)
+
+    def sum_near(t, n, q, h):
+        rows = piece_of(h)
+        return make(3, t, near_out.at[t, n, q, rows], near_in.at[t, n, q, rows], near_sem.at[n, q, h], near[q])
+
+    def sum_over(t, h):
+        rows = piece_of(h)
+        return make(4, t, cross_out.at[t, rows], cross_in.at[t, rows], cross_sem.at[h], over)
+
+    def coef_mine(t, q):
+        return make(5, t, coefb.at[t, s], coefb.at[t, s], mine_sem.at[q], near[q])
+
+    def coef_over(t, h):
+        slot = coefb.at[t, s, piece_of(h)]
+        return make(5, t, slot, slot, over_sem.at[h], over)
+
+    def coef_pass(t, q, h):
+        slot = coefb.at[t, z_over * 2 + x, piece_of(h)]
+        return make(5, t, slot, slot, pass_sem.at[q, h], near[q])
+
+    def pick(t):
+        chosen = picks_ref[t:t + 1, :] - s * pool_dev
+        rows = lax.broadcasted_iota(jnp.int32, (pool_dev, batch), 0)
+        hot = jnp.where(rows == chosen, -2.0, 0.0).astype(jnp.bfloat16)
+        got = jnp.dot(pool_ref[...], hot, preferred_element_type=jnp.float32)
+        feats[t, c] = got.T.astype(jnp.bfloat16)
+        return hot
+
+    def pick_labels(t, hot):
+        label_rows = jnp.broadcast_to(labels_ref[...].astype(jnp.float32), (16, pool_dev)).astype(jnp.bfloat16)
+        lab = -0.5 * jnp.dot(label_rows, hot, preferred_element_type=jnp.float32)
+        for n in range(2 * CHUNKS):
+            labs[t, n] = lab[0:8, n * half:(n + 1) * half]
+
+    bend = (1.0 / (LENGTH_SCALE * math.log(2.0))) ** 2
+
+    def laplace(t, i, first, last):
+        rows = rows_of(i)
+        ssq = sum(
+            jnp.sum(jnp.square(feats[t, q, rows].astype(jnp.float32)), axis=1, keepdims=True) for q in range(4)
+        ) * 0.25
+
+        def body(j, _):
+            cols = pl.ds(pl.multiple_of(j * tile, tile), tile)
+            lhs = jnp.concatenate([feats[t, q, rows] for q in range(4)], axis=1)
+            cross = jnp.dot(lhs, cen[:, cols], preferred_element_type=jnp.float32)
+            arg = ((ssq + csq[:, cols]) + cross) * (bend / width) + bend * EPS
+            arg = jnp.maximum(arg, 1e-30)
+            value = jnp.exp2(-(arg * lax.rsqrt(arg)))
+            for q in range(2):
+                kern[t, j * 2 + q, rows] = value[:, q * own:(q + 1) * own].astype(jnp.bfloat16)
+            return 0
+
+        lax.fori_loop(first, last, body, 0)
+
+    def logits(t, i, group, first, last):
+        part = sum(
+            lax.dot_general(coefb[t, j], kern[t, j, rows_of(i)], NT, preferred_element_type=jnp.float32)
+            for j in group
+        )
+        if not first:
+            part = part + lacc[i]
+        if not last:
+            lacc[i] = part
+            return
+        for h in range(2):
+            lpart[t, i, h] = part[:, h * half:(h + 1) * half]
+        log_sib(t, i).start()
+
+    def chip_sum(t, i):
+        log_sib(t, i).wait_recv()
+        lsum[t, i] = lpart[t, i, k] + lrecv[t, i]
+        log_far(t, i).start()
+
+    def residual(t, i):
+        log_far(t, i).wait_recv()
+        value = (lsum[t, i] + ysum[t, i]) * logit_scale
+        expo = jnp.exp(value - jnp.max(value, axis=0, keepdims=True))
+        probs = expo / jnp.sum(expo, axis=0, keepdims=True)
+        ids = lax.broadcasted_iota(jnp.int32, (classes, half), 0).astype(jnp.float32)
+        hot = jnp.where(ids == labs[t, 2 * i + k][0:1, :], 1.0, 0.0)
+        resid[t, i, k] = (probs - hot).astype(jnp.bfloat16)
+        res_sib(t, i).start()
+
+    def gradient(t):
+        for i in range(CHUNKS):
+            res_sib(t, i).wait_recv()
+        whole = jnp.concatenate([resid[t, i, h] for i in range(CHUNKS) for h in range(2)], axis=1)
+
+        def grad(block):
+            return jnp.dot(whole, kern[t, block], preferred_element_type=jnp.float32)
+
+        parts = [grad(block) for block in across]
+        for h in range(PIECES):
+            for q in range(3):
+                near_out[t, 0, q, piece_of(h)] = encode(parts[q][piece_of(h)])
+                sum_near(t, 0, q, h).start()
+        for q in range(3):
+            near_out[t, 1, q] = encode(grad(quad[q]))
+            for h in range(PIECES):
+                sum_near(t, 1, q, h).start()
+        gown[0] = grad(z_over * 2 + x)
+        gown[1] = grad(s)
+
+    def reduce_near(t, n, h):
+        total = gown[n, piece_of(h)]
+        for q in range(3):
+            sum_near(t, n, q, h).wait_recv()
+            total = total + decode(near_in[t, n, q, piece_of(h)])
+        return total
+
+    def reduce_across(t, h):
+        cross_out[t, piece_of(h)] = encode(reduce_near(t, 0, h))
+        sum_over(t, h).start()
+
+    def reduce_end(t, h):
+        total = reduce_near(t, 1, h)
+        sum_over(t, h).wait_recv()
+        return total + decode(cross_in[t, piece_of(h)])
+
+    def share_mine(t):
+        for h in range(PIECES):
+            coef_over(t, h).start()
+        for q in range(3):
+            coef_mine(t, q).start()
+
+    def share_pass(t, h):
+        coef_over(t, h).wait_recv()
+        for q in range(3):
+            coef_pass(t, q, h).start()
+
+    def share_near(t):
+        for q in range(3):
+            coef_mine(t, q).wait_recv()
+
+    def share_end(t):
+        for q in range(3):
+            for h in range(PIECES):
+                coef_pass(t, q, h).wait_recv()
+
+    first_group = [s] + quad + [z_over * 2 + x]
+
+    pl.semaphore_wait(barrier, 6)
+    loads[3].wait()
+    coefb[0, s] = cur[...].astype(jnp.bfloat16)
+    share_mine(0)
+    loads[0].wait()
+    loads[1].wait()
+    hots = pick(0)
+    for i in range(CHUNKS):
+        feat_far(0, i).start()
+        feat_sib(0, i).start()
+    loads[2].wait()
+    pick_labels(0, hots)
+    pick_labels(1, pick(1))
+    loads[4].wait()
+
+    def square(j, _):
+        cols = pl.ds(pl.multiple_of(j * own, own), own)
+        block = cen[:, cols].astype(jnp.float32)
+        csq[:, cols] = jnp.sum(block * block, axis=0, keepdims=True)
+        return 0
+
+    lax.fori_loop(0, cen_dev // own, square, 0)
+
+    for h in range(PIECES):
+        share_pass(0, h)
+    feat_far(0, 0).wait_recv()
+    feat_fwd(0, 0).start()
+    feat_sib(0, 0).wait_recv()
+    feat_fwd(0, 0).wait_recv()
+    laplace(0, 0, 0, tiles)
+    feat_far(0, 1).wait_recv()
+    feat_fwd(0, 1).start()
+    share_near(0)
+    share_end(0)
+    logits(0, 0, first_group + across, True, True)
+    feat_sib(0, 1).wait_recv()
+    feat_fwd(0, 1).wait_recv()
+    laplace(0, 1, 0, tiles // 2)
+    chip_sum(0, 0)
+    laplace(0, 1, tiles // 2, tiles)
+    logits(0, 1, first_group + across, True, True)
+    residual(0, 0)
+    chip_sum(0, 1)
+    for i in range(CHUNKS):
+        feat_far(1, i).start()
+        feat_sib(1, i).start()
+    residual(0, 1)
+
+    gradient(0)
+    feat_far(1, 0).wait_recv()
+    feat_fwd(1, 0).start()
+    feat_sib(1, 0).wait_recv()
+    reduce_across(0, 0)
+    feat_fwd(1, 0).wait_recv()
+    reduce_across(0, 1)
+    laplace(1, 0, 0, 1)
+    reduce_across(0, 2)
+    feat_far(1, 1).wait_recv()
+    feat_fwd(1, 1).start()
+    laplace(1, 0, 1, tiles)
+    for h in range(PIECES):
+        rows = piece_of(h)
+        fresh = cur[rows] - rate * reduce_end(0, h)
+        cur[rows] = fresh
+        coefb[1, s, rows] = fresh.astype(jnp.bfloat16)
+        coef_over(1, h).start()
+    for q in range(3):
+        coef_mine(1, q).start()
+    feat_sib(1, 1).wait_recv()
+    feat_fwd(1, 1).wait_recv()
+    laplace(1, 1, 0, tiles)
+    for h in range(PIECES):
+        share_pass(1, h)
+    share_near(1)
+    for i in range(CHUNKS):
+        logits(1, i, first_group, True, False)
+    share_end(1)
+    for i in range(CHUNKS):
+        logits(1, i, across, False, True)
+    for i in range(CHUNKS):
+        chip_sum(1, i)
+    for i in range(CHUNKS):
+        residual(1, i)
+    gradient(1)
+    for h in range(PIECES):
+        reduce_across(1, h)
+    for h in range(PIECES):
+        out_ref[piece_of(h)] = cur[piece_of(h)] - rate * reduce_end(1, h)
+
+    def drain(kind, t, ref):
+        make(kind, t, ref, ref, cross_sem.at[0], over).wait_send()
+
+    for t in range(steps):
+        drain(0, t, feats.at[t, 0:3])
+        drain(1, t, lpart.at[t])
+        drain(2, t, resid.at[t, 0])
+        drain(3, t, near_out.at[t])
+        drain(4, t, cross_out.at[t])
+        drain(5, t, coefb.at[t, 0:7])
+
+
+def line_device(n_c, n_s, centres, pool, labels, picks, coefs):
+    width, cen_dev = centres.shape
+    fd, pool_dev = pool.shape
+    steps, batch = picks.shape
+    classes, own = coefs.shape
+    half = batch // CHUNKS // 2
+    bf16, f32, i16 = jnp.bfloat16, jnp.float32, jnp.int16
+    dma = pltpu.SemaphoreType.DMA
+    return pl.pallas_call(
+        functools.partial(
+            line_kernel, LOGIT_GAIN / (cen_dev * n_c), STEP_GAIN * LOGIT_GAIN / (batch * n_s)
+        ),
+        out_shape=pltpu.VMEM((classes, own), f32),
+        in_specs=[pl.BlockSpec(memory_space=pltpu.HBM)] * 5,
+        out_specs=pl.BlockSpec(memory_space=pltpu.VMEM),
+        scratch_shapes=[
+            pltpu.VMEM((width, cen_dev), bf16),
+            pltpu.VMEM((fd, pool_dev), bf16),
+            pltpu.VMEM((1, pool_dev), jnp.int32),
+            pltpu.VMEM((steps, batch), jnp.int32),
+            pltpu.VMEM((classes, own), f32),
+            pltpu.VMEM((1, cen_dev), f32),
+            pltpu.VMEM((steps, n_c, batch, fd), bf16),
+            pltpu.VMEM((steps, n_s, batch, own), bf16),
+            pltpu.VMEM((steps, 2 * CHUNKS, 8, half), f32),
+            pltpu.VMEM((steps, n_s, classes, own), bf16),
+            pltpu.VMEM((CHUNKS, classes, 2 * half), f32),
+            pltpu.VMEM((steps, CHUNKS, 2, classes, half), f32),
+            pltpu.VMEM((steps, CHUNKS, classes, half), f32),
+            pltpu.VMEM((steps, CHUNKS, classes, half), f32),
+            pltpu.VMEM((steps, CHUNKS, classes, half), f32),
+            pltpu.VMEM((steps, CHUNKS, 2, classes, half), bf16),
+            pltpu.VMEM((2, classes, own), f32),
+            pltpu.VMEM((steps, 2, 3, classes, own), i16),
+            pltpu.VMEM((steps, 2, 3, classes, own), i16),
+            pltpu.VMEM((steps, classes, own), i16),
+            pltpu.VMEM((steps, classes, own), i16),
+            dma((5,)),
+            dma((6, steps)),
+            dma((steps, 3, CHUNKS)),
+            dma((3, steps, CHUNKS)),
+            dma((2, 3, PIECES)),
+            dma((PIECES,)),
+            dma((3,)),
+            dma((PIECES,)),
+            dma((3, PIECES)),
+        ],
+        compiler_params=pltpu.CompilerParams(
+            collective_id=0, has_side_effects=True, vmem_limit_bytes=60 * 1024 * 1024
+        ),
+    )(centres, pool, labels.reshape(1, pool_dev), picks, coefs)
+
+
+def suits_line(mesh, centres, pool, picks, coefs):
+    n_c, n_s = mesh.shape["centre"], mesh.shape["sample"]
+    own, batch, fd = coefs.shape[1], picks.shape[1], pool.shape[0]
+    return (
+        n_c == 4 and n_s == 8 and own % 128 == 0 and fd % 128 == 0 and picks.shape[0] == 2
+        and batch % (256 * CHUNKS) == 0 and coefs.shape[0] % (16 * PIECES) == 0 and batch * n_s <= 4096
+    )
+
+
+def on_device(mesh, centres, pool, labels, picks, coefs):
+    n_c, n_s = mesh.shape["centre"], mesh.shape["sample"]
+    if suits_line(mesh, centres, pool, picks, coefs):
+        return line_device(n_c, n_s, centres, pool, labels, picks, coefs)
     width, cen_dev = centres.shape
     fd, pool_dev = pool.shape
     steps, batch = picks.shape
@@ -283,7 +688,7 @@
         P(None, ("centre", "sample")),
     )
     return jax.shard_map(
-        functools.partial(on_device, mesh.shape["centre"], mesh.shape["sample"]),
+        functools.partial(on_device, mesh),
         mesh=mesh,
         in_specs=placed,
         out_specs=P(None, ("centre", "sample")),

time: 81.5 us -> 66 us (0.81)
  Pallas kernels: 79.2 us -> 65.2 us
  local copies, waits for them, and re-layouts: 1.58 us -> 0.66 us
    pallas_call x1, Pallas kernels: 79.2 us -> 65.2 us  [line_device(): pl.pallas_call(functools.partial(line_kernel, LOGIT_GAIN / (cen_dev * n_c...]
    unnamed x1, local copies, waits for them, and re-layouts: 1.58 us -> 0.66 us
where the time goes in v2:
time: 66 us; the launch traced here: 65.8 us
  Pallas kernels  65.2 us (99%)
  local copies, waits for them, and re-layouts  0.66 us (1%)
    pallas_call x1, Pallas kernels, line_device(): pl.pallas_call(functools.partial(line_kernel, LOGIT_GAIN / (cen_dev * n_c...  65.2 us

profile of v2, /device:TPU:0, one launch (start us, length us, event | category | flops | bytes accessed | tf_op | source)
XLA Modules:
  0.0 65.8 jit_solution(16427106864268812631)
XLA Ops:
  0.0 65.2 %shard_map.55 = f32[144,256]{1,0:T(8,128)S(1)} custom-call(bf16[1024,2048]{1,0:T(8,128)(2,1)} %cen_hbm.1, bf16[256,1024]{1,0:T(8,128)(2,1)} %pool_hbm.1, s32[1,1024]{1,0:T(1,128)} %bitcast.1, s32[2,512]{1,0:T(2,128)} %picks_hbm.1, f32[144,256]{1,0:T(8,128)} %coefs_hbm.1), custom_call_target="tpu_custom_call" | custom-call | tf_op jit(solution)/shard_map/pallas_call | solution.py:580
  65.2 0.7 %copy.7 = f32[144,256]{1,0:T(8,128)} copy(f32[144,256]{1,0:T(8,128)S(1)} %shard_map.55) | data formatting | bytes 294912

commit v3 on v2

--- a/solution.py
+++ b/solution.py
@@ -233,6 +233,8 @@
 PIECES = 3
 LOG_STEPS = 520.0
 LOG_LOW = 50.0
+LEVELS = 64.0
+FIXED = 32000.0
 
 
 def encode(value):
@@ -251,7 +253,7 @@
     logit_scale, rate,
     cen_hbm, pool_hbm, labels_hbm, picks_hbm, coefs_hbm, out_ref,
     cen, pool_ref, labels_ref, picks_ref, cur,
-    csq, feats, kern, labs, coefb, lacc, lpart, lrecv, lsum, ysum, resid, gown,
+    csq, feats, kern, labs, coefb, lacc, lpart, lrecv, lsum, ysend, ysum, resid, gown,
     near_out, near_in, cross_out, cross_in,
     load_sem, send_sem, feat_sem, log_sem, near_sem, cross_sem, mine_sem, over_sem, pass_sem,
 ):
@@ -322,7 +324,7 @@
         return make(1, t, lpart.at[t, i, 1 - k], lrecv.at[t, i], log_sem.at[0, t, i], sib)
 
     def log_far(t, i):
-        return make(1, t, lsum.at[t, i], ysum.at[t, i], log_sem.at[1, t, i], far)
+        return make(6, t, ysend.at[t, i], ysum.at[t, i], log_sem.at[1, t, i], far)
 
     def res_sib(t, i):
         return make(2, t, resid.at[t, i, k], resid.at[t, i, k], log_sem.at[2, t, i], sib)
@@ -335,8 +337,9 @@
         rows = piece_of(h)
         return make(4, t, cross_out.at[t, rows], cross_in.at[t, rows], cross_sem.at[h], over)
 
-    def coef_mine(t, q):
-        return make(5, t, coefb.at[t, s], coefb.at[t, s], mine_sem.at[q], near[q])
+    def coef_mine(t, q, h=None):
+        slot = coefb.at[t, s] if h is None else coefb.at[t, s, piece_of(h)]
+        return make(5, t, slot, slot, mine_sem.at[q], near[q])
 
     def coef_over(t, h):
         slot = coefb.at[t, s, piece_of(h)]
@@ -346,19 +349,19 @@
         slot = coefb.at[t, z_over * 2 + x, piece_of(h)]
         return make(5, t, slot, slot, pass_sem.at[q, h], near[q])
 
-    def pick(t):
-        chosen = picks_ref[t:t + 1, :] - s * pool_dev
-        rows = lax.broadcasted_iota(jnp.int32, (pool_dev, batch), 0)
+    def pick(t, i):
+        chosen = picks_ref[t:t + 1, rows_of(i)] - s * pool_dev
+        rows = lax.broadcasted_iota(jnp.int32, (pool_dev, rows_n), 0)
         hot = jnp.where(rows == chosen, -2.0, 0.0).astype(jnp.bfloat16)
         got = jnp.dot(pool_ref[...], hot, preferred_element_type=jnp.float32)
-        feats[t, c] = got.T.astype(jnp.bfloat16)
+        feats[t, c, rows_of(i)] = got.T.astype(jnp.bfloat16)
         return hot
 
-    def pick_labels(t, hot):
+    def pick_labels(t, i, hot):
         label_rows = jnp.broadcast_to(labels_ref[...].astype(jnp.float32), (16, pool_dev)).astype(jnp.bfloat16)
         lab = -0.5 * jnp.dot(label_rows, hot, preferred_element_type=jnp.float32)
-        for n in range(2 * CHUNKS):
-            labs[t, n] = lab[0:8, n * half:(n + 1) * half]
+        for h in range(2):
+            labs[t, 2 * i + h] = lab[0:8, h * half:(h + 1) * half]
 
     bend = (1.0 / (LENGTH_SCALE * math.log(2.0))) ** 2
 
@@ -397,12 +400,20 @@
 
     def chip_sum(t, i):
         log_sib(t, i).wait_recv()
-        lsum[t, i] = lpart[t, i, k] + lrecv[t, i]
+        value = lpart[t, i, k] + lrecv[t, i]
+        lsum[t, i] = value
+        top = jnp.maximum(jnp.max(jnp.abs(value), axis=0, keepdims=True), 2.0 ** -100)
+        level = jnp.ceil(jnp.log(top) * (LEVELS / math.log(2.0)))
+        code = jnp.round(value * (FIXED * jnp.exp2(level * (-1.0 / LEVELS))))
+        ysend[t, i, 0:classes] = code.astype(jnp.int16)
+        ysend[t, i, classes:] = jnp.broadcast_to(level, (16, half)).astype(jnp.int16)
         log_far(t, i).start()
 
     def residual(t, i):
         log_far(t, i).wait_recv()
-        value = (lsum[t, i] + ysum[t, i]) * logit_scale
+        level = ysum[t, i, classes:].astype(jnp.float32)[0:1]
+        other = ysum[t, i, 0:classes].astype(jnp.float32) * (jnp.exp2(level * (1.0 / LEVELS)) * (1.0 / FIXED))
+        value = (lsum[t, i] + other) * logit_scale
         expo = jnp.exp(value - jnp.max(value, axis=0, keepdims=True))
         probs = expo / jnp.sum(expo, axis=0, keepdims=True)
         ids = lax.broadcasted_iota(jnp.int32, (classes, half), 0).astype(jnp.float32)
@@ -420,12 +431,13 @@
 
         parts = [grad(block) for block in across]
         for h in range(PIECES):
-            for q in range(3):
+            for q in (2, 1, 0):
                 near_out[t, 0, q, piece_of(h)] = encode(parts[q][piece_of(h)])
                 sum_near(t, 0, q, h).start()
-        for q in range(3):
-            near_out[t, 1, q] = encode(grad(quad[q]))
-            for h in range(PIECES):
+        parts = [grad(block) for block in quad]
+        for h in range(PIECES):
+            for q in (2, 1, 0):
+                near_out[t, 1, q, piece_of(h)] = encode(parts[q][piece_of(h)])
                 sum_near(t, 1, q, h).start()
         gown[0] = grad(z_over * 2 + x)
         gown[1] = grad(s)
@@ -454,7 +466,7 @@
 
     def share_pass(t, h):
         coef_over(t, h).wait_recv()
-        for q in range(3):
+        for q in (2, 1, 0):
             coef_pass(t, q, h).start()
 
     def share_near(t):
@@ -474,13 +486,16 @@
     share_mine(0)
     loads[0].wait()
     loads[1].wait()
-    hots = pick(0)
+    hots = []
     for i in range(CHUNKS):
+        hots.append(pick(0, i))
         feat_far(0, i).start()
         feat_sib(0, i).start()
     loads[2].wait()
-    pick_labels(0, hots)
-    pick_labels(1, pick(1))
+    for i in range(CHUNKS):
+        pick_labels(0, i, hots[i])
+    for i in range(CHUNKS):
+        pick_labels(1, i, pick(1, i))
     loads[4].wait()
 
     def square(j, _):
@@ -500,20 +515,20 @@
     laplace(0, 0, 0, tiles)
     feat_far(0, 1).wait_recv()
     feat_fwd(0, 1).start()
+    feat_sib(0, 1).wait_recv()
+    feat_fwd(0, 1).wait_recv()
+    laplace(0, 1, 0, tiles // 2)
     share_near(0)
     share_end(0)
     logits(0, 0, first_group + across, True, True)
-    feat_sib(0, 1).wait_recv()
-    feat_fwd(0, 1).wait_recv()
-    laplace(0, 1, 0, tiles // 2)
+    laplace(0, 1, tiles // 2, tiles)
     chip_sum(0, 0)
-    laplace(0, 1, tiles // 2, tiles)
     logits(0, 1, first_group + across, True, True)
-    residual(0, 0)
     chip_sum(0, 1)
     for i in range(CHUNKS):
         feat_far(1, i).start()
         feat_sib(1, i).start()
+    residual(0, 0)
     residual(0, 1)
 
     gradient(0)
@@ -534,8 +549,8 @@
         cur[rows] = fresh
         coefb[1, s, rows] = fresh.astype(jnp.bfloat16)
         coef_over(1, h).start()
-    for q in range(3):
-        coef_mine(1, q).start()
+        for q in (2, 1, 0):
+            coef_mine(1, q, h).start()
     feat_sib(1, 1).wait_recv()
     feat_fwd(1, 1).wait_recv()
     laplace(1, 1, 0, tiles)
@@ -562,7 +577,8 @@
 
     for t in range(steps):
         drain(0, t, feats.at[t, 0:3])
-        drain(1, t, lpart.at[t])
+        drain(1, t, lpart.at[t, 0])
+        drain(6, t, ysend.at[t])
         drain(2, t, resid.at[t, 0])
         drain(3, t, near_out.at[t])
         drain(4, t, cross_out.at[t])
@@ -599,7 +615,8 @@
             pltpu.VMEM((steps, CHUNKS, 2, classes, half), f32),
             pltpu.VMEM((steps, CHUNKS, classes, half), f32),
             pltpu.VMEM((steps, CHUNKS, classes, half), f32),
-            pltpu.VMEM((steps, CHUNKS, classes, half), f32),
+            pltpu.VMEM((steps, CHUNKS, classes + 16, half), i16),
+            pltpu.VMEM((steps, CHUNKS, classes + 16, half), i16),
             pltpu.VMEM((steps, CHUNKS, 2, classes, half), bf16),
             pltpu.VMEM((2, classes, own), f32),
             pltpu.VMEM((steps, 2, 3, classes, own), i16),
@@ -607,7 +624,7 @@
             pltpu.VMEM((steps, classes, own), i16),
             pltpu.VMEM((steps, classes, own), i16),
             dma((5,)),
-            dma((6, steps)),
+            dma((7, steps)),
             dma((steps, 3, CHUNKS)),
             dma((3, steps, CHUNKS)),
             dma((2, 3, PIECES)),

time: 66 us -> 61.4 us (0.930)
  Pallas kernels: 65.2 us -> 60.6 us
    pallas_call x1, Pallas kernels: 65.2 us -> 60.6 us  [line_device(): pl.pallas_call(functools.partial(line_kernel, LOGIT_GAIN / (cen_dev * n_c...]
where the time goes in v3:
time: 61.4 us; the launch traced here: 61.2 us
  Pallas kernels  60.6 us (99%)
  local copies, waits for them, and re-layouts  0.66 us (1%)
    pallas_call x1, Pallas kernels, line_device(): pl.pallas_call(functools.partial(line_kernel, LOGIT_GAIN / (cen_dev * n_c...  60.6 us

profile of v3, /device:TPU:0, one launch (start us, length us, event | category | flops | bytes accessed | tf_op | source)
XLA Modules:
  0.0 61.2 jit_solution(9787499975371516168)
XLA Ops:
  0.0 60.6 %shard_map.55 = f32[144,256]{1,0:T(8,128)S(1)} custom-call(bf16[1024,2048]{1,0:T(8,128)(2,1)} %cen_hbm.1, bf16[256,1024]{1,0:T(8,128)(2,1)} %pool_hbm.1, s32[1,1024]{1,0:T(1,128)} %bitcast.1, s32[2,512]{1,0:T(2,128)} %picks_hbm.1, f32[144,256]{1,0:T(8,128)} %coefs_hbm.1), custom_call_target="tpu_custom_call" | custom-call | tf_op jit(solution)/shard_map/pallas_call | solution.py:596
  60.6 0.7 %copy.7 = f32[144,256]{1,0:T(8,128)} copy(f32[144,256]{1,0:T(8,128)S(1)} %shard_map.55) | data formatting | bytes 294912

commit v4 on v3

--- a/solution.py
+++ b/solution.py
@@ -253,7 +253,7 @@
     logit_scale, rate,
     cen_hbm, pool_hbm, labels_hbm, picks_hbm, coefs_hbm, out_ref,
     cen, pool_ref, labels_ref, picks_ref, cur,
-    csq, feats, kern, labs, coefb, lacc, lpart, lrecv, lsum, ysend, ysum, resid, gown,
+    csq, part, feats, kern, labs, coefb, lacc, lpart, lrecv, lsum, ysend, ysum, resid, gown,
     near_out, near_in, cross_out, cross_in,
     load_sem, send_sem, feat_sem, log_sem, near_sem, cross_sem, mine_sem, over_sem, pass_sem,
 ):
@@ -292,7 +292,7 @@
             [(picks_hbm, picks_ref), (pool_hbm, pool_ref), (labels_hbm, labels_ref), (coefs_hbm, cur), (cen_hbm, cen)]
         )
     ]
-    for i in (3, 0, 1, 2, 4):
+    for i in (0, 1, 3, 2, 4):
         loads[i].start()
 
     def make(kind, t, src, dst, recv, peer):
@@ -382,7 +382,45 @@
                 kern[t, j * 2 + q, rows] = value[:, q * own:(q + 1) * own].astype(jnp.bfloat16)
             return 0
 
-        lax.fori_loop(first, last, body, 0)
+        lax.fori_loop(first, last, body, 0, unroll=min(2, last - first))
+
+    def near_part(i):
+        rows = rows_of(i)
+        slots = (2 * y, 2 * y + 1)
+        ssq = sum(
+            jnp.sum(jnp.square(feats[0, q, rows].astype(jnp.float32)), axis=1, keepdims=True) for q in slots
+        ) * 0.25
+
+        def body(j, _):
+            cols = pl.ds(pl.multiple_of(j * tile, tile), tile)
+            lhs = jnp.concatenate([feats[0, q, rows] for q in slots], axis=1)
+            deep = pl.ds(pl.multiple_of(2 * y * fd, 2 * fd), 2 * fd)
+            cross = jnp.dot(lhs, cen[deep, cols], preferred_element_type=jnp.float32)
+            part[rows, cols] = (ssq + csq[:, cols]) + cross
+            return 0
+
+        lax.fori_loop(0, tiles, body, 0, unroll=2)
+
+    def laplace_far(i, first, last):
+        rows = rows_of(i)
+        slots = (2 * (1 - y), 2 * (1 - y) + 1)
+        ssq = sum(
+            jnp.sum(jnp.square(feats[0, q, rows].astype(jnp.float32)), axis=1, keepdims=True) for q in slots
+        ) * 0.25
+
+        def body(j, _):
+            cols = pl.ds(pl.multiple_of(j * tile, tile), tile)
+            lhs = jnp.concatenate([feats[0, q, rows] for q in slots], axis=1)
+            deep = pl.ds(pl.multiple_of(2 * (1 - y) * fd, 2 * fd), 2 * fd)
+            cross = jnp.dot(lhs, cen[deep, cols], preferred_element_type=jnp.float32)
+            arg = ((part[rows, cols] + ssq) + cross) * (bend / width) + bend * EPS
+            arg = jnp.maximum(arg, 1e-30)
+            value = jnp.exp2(-(arg * lax.rsqrt(arg)))
+            for q in range(2):
+                kern[0, j * 2 + q, rows] = value[:, q * own:(q + 1) * own].astype(jnp.bfloat16)
+            return 0
+
+        lax.fori_loop(first, last, body, 0, unroll=min(2, last - first))
 
     def logits(t, i, group, first, last):
         part = sum(
@@ -473,10 +511,9 @@
         for q in range(3):
             coef_mine(t, q).wait_recv()
 
-    def share_end(t):
-        for q in range(3):
-            for h in range(PIECES):
-                coef_pass(t, q, h).wait_recv()
+    def share_end(t, q):
+        for h in range(PIECES):
+            coef_pass(t, q, h).wait_recv()
 
     first_group = [s] + quad + [z_over * 2 + x]
 
@@ -506,22 +543,27 @@
 
     lax.fori_loop(0, cen_dev // own, square, 0)
 
-    for h in range(PIECES):
+    feat_sib(0, 0).wait_recv()
+    near_part(0)
+    share_pass(0, 0)
+    feat_sib(0, 1).wait_recv()
+    near_part(1)
+    for h in range(1, PIECES):
         share_pass(0, h)
     feat_far(0, 0).wait_recv()
     feat_fwd(0, 0).start()
-    feat_sib(0, 0).wait_recv()
     feat_fwd(0, 0).wait_recv()
-    laplace(0, 0, 0, tiles)
+    laplace_far(0, 0, tiles // 2)
     feat_far(0, 1).wait_recv()
     feat_fwd(0, 1).start()
-    feat_sib(0, 1).wait_recv()
+    laplace_far(0, tiles // 2, tiles)
     feat_fwd(0, 1).wait_recv()
-    laplace(0, 1, 0, tiles // 2)
+    laplace_far(1, 0, tiles // 2)
     share_near(0)
-    share_end(0)
+    for q in range(3):
+        share_end(0, q)
     logits(0, 0, first_group + across, True, True)
-    laplace(0, 1, tiles // 2, tiles)
+    laplace_far(1, tiles // 2, tiles)
     chip_sum(0, 0)
     logits(0, 1, first_group + across, True, True)
     chip_sum(0, 1)
@@ -559,9 +601,10 @@
     share_near(1)
     for i in range(CHUNKS):
         logits(1, i, first_group, True, False)
-    share_end(1)
-    for i in range(CHUNKS):
-        logits(1, i, across, False, True)
+    for q in range(3):
+        share_end(1, q)
+        for i in range(CHUNKS):
+            logits(1, i, across[q:q + 1], False, q == 2)
     for i in range(CHUNKS):
         chip_sum(1, i)
     for i in range(CHUNKS):
@@ -607,6 +650,7 @@
             pltpu.VMEM((steps, batch), jnp.int32),
             pltpu.VMEM((classes, own), f32),
             pltpu.VMEM((1, cen_dev), f32),
+            pltpu.VMEM((batch, cen_dev), f32),
             pltpu.VMEM((steps, n_c, batch, fd), bf16),
             pltpu.VMEM((steps, n_s, batch, own), bf16),
             pltpu.VMEM((steps, 2 * CHUNKS, 8, half), f32),

time: 61.4 us -> 59.2 us (0.964)
  Pallas kernels: 60.6 us -> 58.4 us
    pallas_call x1, Pallas kernels: 60.6 us -> 58.4 us  [line_device(): pl.pallas_call(functools.partial(line_kernel, LOGIT_GAIN / (cen_dev * n_c...]
where the time goes in v4:
time: 59.2 us; the launch traced here: 59.1 us
  Pallas kernels  58.4 us (99%)
  local copies, waits for them, and re-layouts  0.66 us (1%)
    pallas_call x1, Pallas kernels, line_device(): pl.pallas_call(functools.partial(line_kernel, LOGIT_GAIN / (cen_dev * n_c...  58.4 us

profile of v4, /device:TPU:0, one launch (start us, length us, event | category | flops | bytes accessed | tf_op | source)
XLA Modules:
  0.0 59.1 jit_solution(11404115225525754734)
XLA Ops:
  0.0 58.4 %shard_map.55 = f32[144,256]{1,0:T(8,128)S(1)} custom-call(bf16[1024,2048]{1,0:T(8,128)(2,1)} %cen_hbm.1, bf16[256,1024]{1,0:T(8,128)(2,1)} %pool_hbm.1, s32[1,1024]{1,0:T(1,128)} %bitcast.1, s32[2,512]{1,0:T(2,128)} %picks_hbm.1, f32[144,256]{1,0:T(8,128)} %coefs_hbm.1), custom_call_target="tpu_custom_call" | custom-call | tf_op jit(solution)/shard_map/pallas_call | solution.py:639
  58.4 0.7 %copy.7 = f32[144,256]{1,0:T(8,128)} copy(f32[144,256]{1,0:T(8,128)S(1)} %shard_map.55) | data formatting | bytes 294912

commit v5 on v4

--- a/solution.py
+++ b/solution.py
@@ -266,6 +266,7 @@
     piece = classes // PIECES
     tile = 2 * own
     tiles = cen_dev // tile
+    blocks = cen_dev // own
 
     c = lax.axis_index("centre")
     s = lax.axis_index("sample")
@@ -297,7 +298,7 @@
 
     def make(kind, t, src, dst, recv, peer):
         return pltpu.make_async_remote_copy(
-            src_ref=src, dst_ref=dst, send_sem=send_sem.at[kind, t], recv_sem=recv,
+            src_ref=src, dst_ref=dst, send_sem=send_sem.at[kind], recv_sem=recv,
             device_id=peer, device_id_type=MESH,
         )
 
@@ -423,17 +424,17 @@
         lax.fori_loop(first, last, body, 0, unroll=min(2, last - first))
 
     def logits(t, i, group, first, last):
-        part = sum(
+        total = sum(
             lax.dot_general(coefb[t, j], kern[t, j, rows_of(i)], NT, preferred_element_type=jnp.float32)
             for j in group
         )
         if not first:
-            part = part + lacc[i]
+            total = total + lacc[i]
         if not last:
-            lacc[i] = part
+            lacc[i] = total
             return
         for h in range(2):
-            lpart[t, i, h] = part[:, h * half:(h + 1) * half]
+            lpart[t, i, h] = total[:, h * half:(h + 1) * half]
         log_sib(t, i).start()
 
     def chip_sum(t, i):
@@ -558,19 +559,18 @@
     feat_fwd(0, 1).start()
     laplace_far(0, tiles // 2, tiles)
     feat_fwd(0, 1).wait_recv()
-    laplace_far(1, 0, tiles // 2)
+    laplace_far(1, 0, tiles)
     share_near(0)
     for q in range(3):
         share_end(0, q)
-    logits(0, 0, first_group + across, True, True)
-    laplace_far(1, tiles // 2, tiles)
-    chip_sum(0, 0)
-    logits(0, 1, first_group + across, True, True)
-    chip_sum(0, 1)
+    for i in range(CHUNKS):
+        logits(0, i, range(blocks), True, True)
+    for i in range(CHUNKS):
+        chip_sum(0, i)
+    residual(0, 0)
     for i in range(CHUNKS):
         feat_far(1, i).start()
         feat_sib(1, i).start()
-    residual(0, 0)
     residual(0, 1)
 
     gradient(0)
@@ -615,17 +615,16 @@
     for h in range(PIECES):
         out_ref[piece_of(h)] = cur[piece_of(h)] - rate * reduce_end(1, h)
 
-    def drain(kind, t, ref):
-        make(kind, t, ref, ref, cross_sem.at[0], over).wait_send()
-
-    for t in range(steps):
-        drain(0, t, feats.at[t, 0:3])
-        drain(1, t, lpart.at[t, 0])
-        drain(6, t, ysend.at[t])
-        drain(2, t, resid.at[t, 0])
-        drain(3, t, near_out.at[t])
-        drain(4, t, cross_out.at[t])
-        drain(5, t, coefb.at[t, 0:7])
+    def drain(kind, ref):
+        make(kind, 0, ref, ref, cross_sem.at[0], over).wait_send()
+
+    drain(0, feats.at[:, 0:3])
+    drain(1, lpart.at[:, 0])
+    drain(2, resid.at[:, 0])
+    drain(3, near_out)
+    drain(4, cross_out)
+    drain(5, coefb.at[:, 0:7])
+    drain(6, ysend)
 
 
 def line_device(n_c, n_s, centres, pool, labels, picks, coefs):
@@ -668,7 +667,7 @@
             pltpu.VMEM((steps, classes, own), i16),
             pltpu.VMEM((steps, classes, own), i16),
             dma((5,)),
-            dma((7, steps)),
+            dma((7,)),
             dma((steps, 3, CHUNKS)),
             dma((3, steps, CHUNKS)),
             dma((2, 3, PIECES)),

time: 59.2 us -> 58.6 us (0.990)
  Pallas kernels: 58.4 us -> 57.8 us
    pallas_call x1, Pallas kernels: 58.4 us -> 57.8 us  [line_device(): pl.pallas_call(functools.partial(line_kernel, LOGIT_GAIN / (cen_dev * n_c...]
where the time goes in v5:
time: 58.6 us; the launch traced here: 58.5 us
  Pallas kernels  57.8 us (99%)
  local copies, waits for them, and re-layouts  0.66 us (1%)
    pallas_call x1, Pallas kernels, line_device(): pl.pallas_call(functools.partial(line_kernel, LOGIT_GAIN / (cen_dev * n_c...  57.8 us

profile of v5, /device:TPU:0, one launch (start us, length us, event | category | flops | bytes accessed | tf_op | source)
XLA Modules:
  0.0 58.5 jit_solution(459452334457090926)
XLA Ops:
  0.0 57.8 %shard_map.55 = f32[144,256]{1,0:T(8,128)S(1)} custom-call(bf16[1024,2048]{1,0:T(8,128)(2,1)} %cen_hbm.1, bf16[256,1024]{1,0:T(8,128)(2,1)} %pool_hbm.1, s32[1,1024]{1,0:T(1,128)} %bitcast.1, s32[2,512]{1,0:T(2,128)} %picks_hbm.1, f32[144,256]{1,0:T(8,128)} %coefs_hbm.1), custom_call_target="tpu_custom_call" | custom-call | tf_op jit(solution)/shard_map/pallas_call | solution.py:638
  57.8 0.7 %copy.7 = f32[144,256]{1,0:T(8,128)} copy(f32[144,256]{1,0:T(8,128)S(1)} %shard_map.55) | data formatting | bytes 294912

commit v6 on v5

--- a/solution.py
+++ b/solution.py
@@ -383,7 +383,7 @@
                 kern[t, j * 2 + q, rows] = value[:, q * own:(q + 1) * own].astype(jnp.bfloat16)
             return 0
 
-        lax.fori_loop(first, last, body, 0, unroll=min(2, last - first))
+        lax.fori_loop(first, last, body, 0, unroll=last - first)
 
     def near_part(i):
         rows = rows_of(i)
@@ -400,7 +400,7 @@
             part[rows, cols] = (ssq + csq[:, cols]) + cross
             return 0
 
-        lax.fori_loop(0, tiles, body, 0, unroll=2)
+        lax.fori_loop(0, tiles, body, 0, unroll=tiles)
 
     def laplace_far(i, first, last):
         rows = rows_of(i)
@@ -421,7 +421,7 @@
                 kern[0, j * 2 + q, rows] = value[:, q * own:(q + 1) * own].astype(jnp.bfloat16)
             return 0
 
-        lax.fori_loop(first, last, body, 0, unroll=min(2, last - first))
+        lax.fori_loop(first, last, body, 0, unroll=last - first)
 
     def logits(t, i, group, first, last):
         total = sum(

time: 58.6 us -> 58.3 us (level)
  no operation moved by 1% of the time
where the time goes in v6:
time: 58.3 us; the launch traced here: 58.1 us
  Pallas kernels  57.5 us (99%)
  local copies, waits for them, and re-layouts  0.66 us (1%)
    pallas_call x1, Pallas kernels, line_device(): pl.pallas_call(functools.partial(line_kernel, LOGIT_GAIN / (cen_dev * n_c...  57.5 us

profile of v6, /device:TPU:0, one launch (start us, length us, event | category | flops | bytes accessed | tf_op | source)
XLA Modules:
  0.0 58.1 jit_solution(8417742953979625860)
XLA Ops:
  0.0 57.5 %shard_map.55 = f32[144,256]{1,0:T(8,128)S(1)} custom-call(bf16[1024,2048]{1,0:T(8,128)(2,1)} %cen_hbm.1, bf16[256,1024]{1,0:T(8,128)(2,1)} %pool_hbm.1, s32[1,1024]{1,0:T(1,128)} %bitcast.1, s32[2,512]{1,0:T(2,128)} %picks_hbm.1, f32[144,256]{1,0:T(8,128)} %coefs_hbm.1), custom_call_target="tpu_custom_call" | custom-call | tf_op jit(solution)/shard_map/pallas_call | solution.py:638
  57.5 0.7 %copy.7 = f32[144,256]{1,0:T(8,128)} copy(f32[144,256]{1,0:T(8,128)S(1)} %shard_map.55) | data formatting | bytes 294912

commit v7 on v6

--- a/solution.py
+++ b/solution.py
@@ -293,7 +293,7 @@
             [(picks_hbm, picks_ref), (pool_hbm, pool_ref), (labels_hbm, labels_ref), (coefs_hbm, cur), (cen_hbm, cen)]
         )
     ]
-    for i in (0, 1, 3, 2, 4):
+    for i in (1, 3, 0, 2):
         loads[i].start()
 
     def make(kind, t, src, dst, recv, peer):
@@ -461,6 +461,13 @@
         res_sib(t, i).start()
 
     def gradient(t):
+        def share(block, h):
+            left = jnp.concatenate([resid[t, i, h] for i in range(CHUNKS)], axis=1)
+            rows = [pl.ds(pl.multiple_of(i * rows_n + h * half, half), half) for i in range(CHUNKS)]
+            right = jnp.concatenate([kern[t, block, r] for r in rows], axis=0)
+            return jnp.dot(left, right, preferred_element_type=jnp.float32)
+
+        parts = [share(block, k) for block in across]
         for i in range(CHUNKS):
             res_sib(t, i).wait_recv()
         whole = jnp.concatenate([resid[t, i, h] for i in range(CHUNKS) for h in range(2)], axis=1)
@@ -468,7 +475,7 @@
         def grad(block):
             return jnp.dot(whole, kern[t, block], preferred_element_type=jnp.float32)
 
-        parts = [grad(block) for block in across]
+        parts = [part + share(block, 1 - k) for part, block in zip(parts, across)]
         for h in range(PIECES):
             for q in (2, 1, 0):
                 near_out[t, 0, q, piece_of(h)] = encode(parts[q][piece_of(h)])
@@ -524,6 +531,7 @@
     share_mine(0)
     loads[0].wait()
     loads[1].wait()
+    loads[4].start()
     hots = []
     for i in range(CHUNKS):
         hots.append(pick(0, i))
@@ -580,11 +588,10 @@
     reduce_across(0, 0)
     feat_fwd(1, 0).wait_recv()
     reduce_across(0, 1)
-    laplace(1, 0, 0, 1)
     reduce_across(0, 2)
     feat_far(1, 1).wait_recv()
     feat_fwd(1, 1).start()
-    laplace(1, 0, 1, tiles)
+    laplace(1, 0, 0, tiles)
     for h in range(PIECES):
         rows = piece_of(h)
         fresh = cur[rows] - rate * reduce_end(0, h)

time: 58.3 us -> 58.3 us (level)
  no operation moved by 1% of the time
where the time goes in v7:
time: 58.3 us; the launch traced here: 58.1 us
  Pallas kernels  57.4 us (98%)
  local copies, waits for them, and re-layouts  0.66 us (1%)
    pallas_call x1, Pallas kernels, line_device(): pl.pallas_call(functools.partial(line_kernel, LOGIT_GAIN / (cen_dev * n_c...  57.4 us

profile of v7, /device:TPU:0, one launch (start us, length us, event | category | flops | bytes accessed | tf_op | source)
XLA Modules:
  0.0 58.1 jit_solution(11489805841795361261)
XLA Ops:
  0.0 57.4 %shard_map.55 = f32[144,256]{1,0:T(8,128)S(1)} custom-call(bf16[1024,2048]{1,0:T(8,128)(2,1)} %cen_hbm.1, bf16[256,1024]{1,0:T(8,128)(2,1)} %pool_hbm.1, s32[1,1024]{1,0:T(1,128)} %bitcast.1, s32[2,512]{1,0:T(2,128)} %picks_hbm.1, f32[144,256]{1,0:T(8,128)} %coefs_hbm.1), custom_call_target="tpu_custom_call" | custom-call | tf_op jit(solution)/shard_map/pallas_call | solution.py:645
  57.5 0.7 %copy.7 = f32[144,256]{1,0:T(8,128)} copy(f32[144,256]{1,0:T(8,128)S(1)} %shard_map.55) | data formatting | bytes 294912
